TPU v7x, 32 devices: a whole 2x2x4 slice. The times are simulated.
32 devices in a mesh: row: 8 (over z, y), col: 4 (over x, core).
Axes of the slice: x: 2, y: 2, z: 4, core: 2. Of those that a mesh axis runs over, the one named last changes fastest.
Arguments:
- weights: float32 [2, 4, 2048, 8, 1024], P(None, None, 'row', None, 'col'), may hold values from -6 to 6
Outputs:
- trailing: float32 [2, 4, 2048, 8, 1024], P(None, None, 'row', None, 'col')
- diagonal: float32 [2, 12], replicated
- superdiag: float32 [2, 12], replicated
All inputs are finite; a program needn't handle non-finite values.
Results may differ from a plain program's by a relative error of at most 0.0003.
Values sent between devices are 32-bit elements; how exact they have to be, the bound alone decides.
A program may use at most 128 MiB of HBM per device.

v0:
```python
import functools

import jax
import jax.numpy as jnp
from jax import lax
from jax.experimental import pallas as pl
from jax.experimental.pallas import tpu as pltpu
from jax.sharding import PartitionSpec as P

STEPS = 6
PANELS = 2
TOTAL = STEPS * PANELS
SLOTS = 16
LANES = 128
MESH = pl.DeviceIdType.MESH


def reflect(leading, squares):
    length = jnp.sqrt(squares)
    divisor = jnp.maximum(leading + length, 1.0)
    factor = (leading + length) / jnp.maximum(length, 1.0)
    return (divisor, factor, -length)


def peers(axis, count):
    me = lax.axis_index(axis)
    return [(lax.rem(me + d, count), lax.rem(me - d + count, count)) for d in range(1, count)]


def positions(length, tile_len, devices, place):
    ids = lax.broadcasted_iota(jnp.int32, (1, length), 1)
    return ids // tile_len * (devices * tile_len) + place * tile_len + ids % tile_len


def pack(batch):
    lane = lax.broadcasted_iota(jnp.int32, (8, LANES), 1)
    tile = jnp.zeros((8, LANES), jnp.float32)
    groups = 2 * SLOTS // 8
    at = 0
    for dots, picked, squares, leading in batch:
        for column in (dots, picked):
            for g in range(groups):
                tile = jnp.where(lane == at, column[g * 8 : (g + 1) * 8], tile)
                at += 1
        for scalar in (squares, leading):
            tile = jnp.where(lane == at, scalar, tile)
            at += 1
    return tile


def unpack(tile, batch_n):
    groups = 2 * SLOTS // 8
    at = 0
    result = []
    for _ in range(batch_n):
        columns = []
        for _ in range(2):
            columns.append(
                jnp.concatenate([tile[:, at + g : at + g + 1] for g in range(groups)], axis=0)
            )
            at += groups
        result.append((columns[0], columns[1], tile[0:1, at : at + 1], tile[0:1, at + 1 : at + 2]))
        at += 2
    return result


def exchange(axis, count, par, big, small, sems):
    send_sem, recv_sem = sems
    me = lax.axis_index(axis)

    def copies(source, target, at):
        return [
            pltpu.make_async_remote_copy(
                src_ref=ref.at[par, source],
                dst_ref=ref.at[par, source],
                send_sem=send_sem.at[which, at],
                recv_sem=recv_sem.at[par, which, source],
                device_id={axis: target},
                device_id_type=MESH,
            )
            for which, ref in enumerate((big, small))
        ]

    sends = []
    for at, (to, _) in enumerate(peers(axis, count)):
        for copy in copies(me, to, at):
            copy.start()
            sends.append(copy)
    for at, (_, source) in enumerate(peers(axis, count)):
        for copy in copies(source, source, at):
            copy.wait_recv()
    for copy in sends:
        copy.wait_send()


def kernel(
    row_n, col_n, tile_len, mats, vx, yu, bid,
    cols, rows, spread, sums, row_big, row_small, col_big, col_small,
    row_send, row_recv, col_send, col_recv, slab_send, slab_recv,
):
    batch_n, height, width = mats.shape
    row_place = lax.axis_index("row")
    col_place = lax.axis_index("col")
    barrier = pltpu.get_barrier_semaphore()
    for axis, count in (("row", row_n), ("col", col_n)):
        for to, _ in peers(axis, count):
            pl.semaphore_signal(barrier, inc=1, device_id={axis: to}, device_id_type=MESH)
    pl.semaphore_wait(barrier, row_n + col_n - 2)

    def slab_copy(ref, axis, which, to, at):
        return pltpu.make_async_remote_copy(
            src_ref=ref,
            dst_ref=ref,
            send_sem=slab_send.at[which, at],
            recv_sem=slab_recv.at[which],
            device_id={axis: to},
            device_id_type=MESH,
        )

    slabs = (("col", col_n, cols, col_place), ("row", row_n, rows, row_place))

    @pl.when(col_place == 0)
    def _():
        for m in range(batch_n):
            for b in range(height // LANES):
                span = pl.ds(b * LANES, LANES)
                cols[m, :, span] = mats[m, span, 0:LANES].T[0:SLOTS]
        for at in range(1, col_n):
            slab_copy(cols, "col", 0, at, at).start()

    @pl.when(row_place == 0)
    def _():
        for m in range(batch_n):
            rows[m] = mats[m, 0:SLOTS, :]
        for at in range(1, row_n):
            slab_copy(rows, "row", 1, at, at).start()

    vx[...] = jnp.zeros_like(vx)
    yu[...] = jnp.zeros_like(yu)
    bid[...] = jnp.zeros_like(bid)

    @pl.when(col_place != 0)
    def _():
        slab_copy(cols, "col", 0, 0, 0).wait_recv()

    grow = positions(height, tile_len, row_n, row_place)
    gcol = positions(width, tile_len, col_n, col_place)
    slot = lax.broadcasted_iota(jnp.int32, (2 * SLOTS, 1), 0)
    lane = lax.broadcasted_iota(jnp.int32, (1, LANES), 1)
    own_row = jnp.where(row_place == 0, lane, -1)
    own_col = jnp.where(col_place == 0, lane, -1)
    row_at = lax.broadcasted_iota(jnp.int32, (8, LANES), 0)
    lane_at = lax.broadcasted_iota(jnp.int32, (8, LANES), 1)

    def full_sum(value):
        return jnp.sum(value, axis=1, keepdims=True)

    def step_body(step, weighs):
        par = lax.rem(step, 2)
        col_pieces = []
        batch = []
        for m in range(batch_n):
            old = vx[m]
            piece = cols[m, pl.ds(step, 1), :] - jnp.sum(weighs[m] * old, axis=0, keepdims=True)
            piece = jnp.where(grow >= step, piece, 0.0)
            batch.append(
                (
                    full_sum(old * piece),
                    full_sum(jnp.where(own_row == step, old[:, 0:LANES], 0.0)),
                    full_sum(piece * piece),
                    full_sum(jnp.where(grow == step, piece, 0.0)),
                )
            )
            col_pieces.append(piece)
            for b in range(height // LANES):
                span = slice(b * LANES, (b + 1) * LANES)
                spread[m, span, :] = jnp.broadcast_to(piece[:, span], (LANES, LANES)).T
        for m in range(batch_n):

            def add_rows(at, total):
                span = pl.ds(pl.multiple_of(at * 8, 8), 8)
                scale = spread[m, span, :]
                return tuple(
                    total[t] + mats[m, span, t * LANES : (t + 1) * LANES] * scale
                    for t in range(width // LANES)
                )

            zeros = tuple(jnp.zeros((8, LANES), jnp.float32) for _ in range(width // LANES))
            total = lax.fori_loop(0, height // 8, add_rows, zeros, unroll=4)
            row_big[par, row_place, m : m + 1, :] = jnp.concatenate(
                [jnp.sum(t, axis=0, keepdims=True) for t in total], axis=1
            )
        row_small[par, row_place] = pack(batch)
        exchange("row", row_n, par, row_big, row_small, (row_send, row_recv))

        @pl.when((row_place != 0) & (step == 0))
        def _():
            slab_copy(rows, "row", 1, 0, 0).wait_recv()

        small = row_small[par, 0]
        trans = row_big[par, 0]
        for s in range(1, row_n):
            small = small + row_small[par, s]
            trans = trans + row_big[par, s]
        small_list = unpack(small, batch_n)
        row_pieces = []
        batch = []
        marks = bid[...]
        for m in range(batch_n):
            dots, picked, squares, leading = small_list[m]
            divisor, factor, bidiag = reflect(leading, squares)
            marks = jnp.where((row_at == m) & (lane_at == step), bidiag, marks)
            remain = 1.0 - leading / divisor
            vx[m, pl.ds(step, 1), :] = jnp.where(grow == step, 1.0, col_pieces[m] / divisor)
            pivot_row = rows[m, pl.ds(step, 1), :]
            old = yu[m]
            weight = dots / divisor + picked * remain
            image = factor * (
                trans[m : m + 1] / divisor
                + pivot_row * remain
                - jnp.sum(weight * old, axis=0, keepdims=True)
            )
            image = jnp.where(gcol > step, image, 0.0)
            yu[m, pl.ds(step, 1), :] = image
            piece = pivot_row - image - jnp.sum(picked * old, axis=0, keepdims=True)
            piece = jnp.where(gcol > step, piece, 0.0)
            new = yu[m]
            batch.append(
                (
                    full_sum(new * piece),
                    full_sum(jnp.where(own_col == step + 1, new[:, 0:LANES], 0.0)),
                    full_sum(piece * piece),
                    full_sum(jnp.where(gcol == step + 1, piece, 0.0)),
                )
            )
            row_pieces.append(piece)
        for m in range(batch_n):
            piece = row_pieces[m]
            scale = [
                jnp.broadcast_to(piece[:, t * LANES : (t + 1) * LANES], (8, LANES))
                for t in range(width // LANES)
            ]

            @pl.loop(0, height // 8, unroll=4)
            def _(at):
                span = pl.ds(pl.multiple_of(at * 8, 8), 8)
                parts = [
                    mats[m, span, t * LANES : (t + 1) * LANES] * scale[t]
                    for t in range(width // LANES)
                ]
                while len(parts) > 1:
                    parts = [
                        parts[i] + parts[i + 1] if i + 1 < len(parts) else parts[i]
                        for i in range(0, len(parts), 2)
                    ]
                sums[m, span, :] = parts[0]

        for m in range(batch_n):
            for b in range(height // LANES):
                span = slice(b * LANES, (b + 1) * LANES)
                col_big[par, col_place, m : m + 1, span] = jnp.sum(
                    sums[m, span, :].T, axis=0, keepdims=True
                )
        col_small[par, col_place] = pack(batch)
        exchange("col", col_n, par, col_big, col_small, (col_send, col_recv))
        small = col_small[par, 0]
        applied = col_big[par, 0]
        for s in range(1, col_n):
            small = small + col_small[par, s]
            applied = applied + col_big[par, s]
        small_list = unpack(small, batch_n)
        later = []
        for m in range(batch_n):
            dots, picked, squares, leading = small_list[m]
            divisor, factor, bidiag = reflect(leading, squares)
            marks = jnp.where((row_at == m) & (lane_at == step + SLOTS), bidiag, marks)
            remain = 1.0 - leading / divisor
            yu[m, pl.ds(SLOTS + step, 1), :] = jnp.where(
                gcol == step + 1, 1.0, row_pieces[m] / divisor
            )
            weight = dots / divisor + picked * remain
            image = factor * (
                applied[m : m + 1] / divisor
                + cols[m, pl.ds(step + 1, 1), :] * remain
                - jnp.sum(weight * vx[m], axis=0, keepdims=True)
            )
            vx[m, pl.ds(SLOTS + step, 1), :] = jnp.where(grow > step, image, 0.0)
            later.append(jnp.where(slot == SLOTS + step, 1.0, picked))
        bid[...] = marks
        return tuple(later)

    none = tuple(jnp.zeros((2 * SLOTS, 1), jnp.float32) for _ in range(batch_n))
    lax.fori_loop(0, TOTAL, step_body, none)

    for which, (axis, count, ref, place) in enumerate(slabs):

        @pl.when(place == 0)
        def _():
            for at in range(1, count):
                slab_copy(ref, axis, which, at, at).wait_send()


def factor_all(mats, row_n, col_n, tile_len):
    batch_n, height, width = mats.shape
    whole = pl.BlockSpec(memory_space=pltpu.VMEM)
    f32 = jnp.float32
    return pl.pallas_call(
        functools.partial(kernel, row_n, col_n, tile_len),
        out_shape=(
            jax.ShapeDtypeStruct((batch_n, 2 * SLOTS, height), f32),
            jax.ShapeDtypeStruct((batch_n, 2 * SLOTS, width), f32),
            jax.ShapeDtypeStruct((8, LANES), f32),
        ),
        in_specs=[whole],
        out_specs=(whole, whole, whole),
        scratch_shapes=[
            pltpu.VMEM((batch_n, SLOTS, height), f32),
            pltpu.VMEM((batch_n, SLOTS, width), f32),
            pltpu.VMEM((batch_n, height, LANES), f32),
            pltpu.VMEM((batch_n, height, LANES), f32),
            pltpu.VMEM((2, row_n, batch_n, width), f32),
            pltpu.VMEM((2, row_n, 8, LANES), f32),
            pltpu.VMEM((2, col_n, batch_n, height), f32),
            pltpu.VMEM((2, col_n, 8, LANES), f32),
            pltpu.SemaphoreType.DMA((2, row_n)),
            pltpu.SemaphoreType.DMA((2, 2, row_n)),
            pltpu.SemaphoreType.DMA((2, col_n)),
            pltpu.SemaphoreType.DMA((2, 2, col_n)),
            pltpu.SemaphoreType.DMA((2, max(row_n, col_n))),
            pltpu.SemaphoreType.DMA((2,)),
        ],
        compiler_params=pltpu.CompilerParams(
            collective_id=0, has_side_effects=True, vmem_limit_bytes=48 * 1024 * 1024
        ),
    )(mats)


def per_device(weights):
    batch_n, row_cycles, tile_len, col_cycles, _ = weights.shape
    height = row_cycles * tile_len
    width = col_cycles * tile_len
    row_n = lax.axis_size("row")
    col_n = lax.axis_size("col")
    mats = weights.reshape(batch_n, height, width)
    vx, yu, bid = factor_all(mats, row_n, col_n, tile_len)
    grow = positions(height, tile_len, row_n, lax.axis_index("row"))[0]
    gcol = positions(width, tile_len, col_n, lax.axis_index("col"))[0]
    inside = (grow[:, None] >= TOTAL) & (gcol[None, :] >= TOTAL)
    update = jnp.einsum("mpr,mpc->mrc", vx, yu, precision=lax.Precision.HIGH)
    trailing = jnp.where(inside[None], mats - update, 0.0).reshape(weights.shape)
    return (trailing, bid[:batch_n, :TOTAL], bid[:batch_n, SLOTS : SLOTS + TOTAL])


def solution(mesh):
    placed = (P(None, None, "row", None, "col"),)
    return jax.shard_map(
        per_device,
        mesh=mesh,
        in_specs=placed,
        out_specs=(P(None, None, "row", None, "col"), P(), P()),
        check_vma=False,
    )
```

profile of v0, /device:TPU:0, one launch (start us, length us, event | category | flops | bytes accessed | tf_op | source)
XLA Modules:
  0.0 254.4 jit_solution(13522067983311633811)
XLA Ops:
  0.7 1.4 broadcast_and_fusion
  2.0 18.0 %reshape.160.mats = f32[2,1024,2048]{2,1,0:T(8,128)} reshape(f32[2,4,256,8,256]{4,3,2,1,0:T(8,128)} %param.1) | data formatting | bytes 33554432 | tf_op jit(solution)/shard_map/reshape | solution.py:344
  20.0 203.2 %shard_map.38 = (f32[2,32,1024]{2,1,0:T(8,128)S(1)}, f32[2,32,2048]{2,1,0:T(8,128)S(1)}, f32[8,128]{1,0:T(8,128)S(1)}) custom-call(f32[2,1024,2048]{2,1,0:T(8,128)} %reshape.160.mats), custom_call_target="tpu_custom_call" | custom-call | tf_op jit(solution)/shard_map/pallas_call | solution.py:307
  223.2 14.8 %subtract_select_fusion = f32[2,1024,2048]{2,1,0:T(8,128)} fusion(f32[2,1024,2048]{2,1,0:T(8,128)} %reshape.160.mats, pred[1024,2048]{1,0:T(8,128)(4,1)S(1)} %broadcast_and_fusion, f32[2,32,1024]{2,1,0:T(8,128)S(1)} %get-tuple-element.6, f32[2,32,2048]{2,1,0:T(8,128)S(1)} %get-tuple-element.7), kind=kOutput, calls=%fused_computation | convolution fusion | flops 813694976 | bytes 36438016 | tf_op jit(solution)/shard_map/mpr,mpc->mrc/dot_general | solution.py:349
  238.0 15.8 %copy.4 = f32[256,8,8,256]{3,2,1,0:T(8,128)} copy(f32[256,8,8,256]{3,1,2,0:T(8,128)} %bitcast.8) | data formatting | bytes 33554432
  253.8 0.6 fusion.22
  (2 shorter events, 0.0 us)
where the time goes:
time: 255 us; the launch traced here: 254 us
  Pallas kernels  203 us (80%)
  local copies, waits for them, and re-layouts  34.4 us (13%)
  matrix products  14.8 us (6%)
    pallas_call x1, Pallas kernels, factor_all(): pl.pallas_call(functools.partial(kernel, row_n, col_n, tile_len), out_sha...  203 us
    reshape x1, local copies, waits for them, and re-layouts, per_device(): mats = weights.reshape(batch_n, height, width)  18 us
    unnamed x1, local copies, waits for them, and re-layouts  15.8 us
    dot_general x1, matrix products, per_device(): update = jnp.einsum('mpr,mpc->mrc', vx, yu, precision=lax.Precision.HIGH)  14.8 us

commit v1 on v0

v1 whole, which is shorter than its diff:
```python
import functools

import jax
import jax.numpy as jnp
from jax import lax
from jax.experimental import pallas as pl
from jax.experimental.pallas import tpu as pltpu
from jax.sharding import PartitionSpec as P

STEPS = 6
PANELS = 2
TOTAL = STEPS * PANELS
SLOTS = 2 * TOTAL
LANES = 128
SUB = 8
ROWS_KEPT = 16
SUPER_AT = 64
MESH = pl.DeviceIdType.MESH
F32 = jnp.float32


def reflect(leading, squares):
    length = jnp.sqrt(squares)
    divisor = jnp.maximum(leading + length, 1.0)
    factor = (leading + length) / jnp.maximum(length, 1.0)
    return (divisor, factor, -length)


def partner(me, d, count):
    if count & (count - 1):
        return lax.rem(me + d, count), lax.rem(me - d + count, count)
    to = me
    bit = 1
    while bit < count:
        if d & bit:
            to = to + bit - 2 * bit * lax.rem(me // bit, 2)
        bit *= 2
    return to, to


def peers(axis, count):
    me = lax.axis_index(axis)
    return [partner(me, d, count) for d in range(count - 1, 0, -1)]


def row_ids(blocks, tile_len, devices, place):
    at = lax.broadcasted_iota(jnp.int32, (blocks, LANES), 0) * LANES
    at = at + lax.broadcasted_iota(jnp.int32, (blocks, LANES), 1)
    return at // tile_len * (devices * tile_len) + place * tile_len + at % tile_len


def col_ids(pieces, tile_len, devices, place):
    cycles = pieces * LANES // tile_len
    q = lax.broadcasted_iota(jnp.int32, (pieces, LANES), 0)
    lane = lax.broadcasted_iota(jnp.int32, (pieces, LANES), 1)
    return q % cycles * (devices * tile_len) + place * tile_len + q // cycles * LANES + lane


def tree(parts):
    while len(parts) > 1:
        parts = [
            parts[i] + parts[i + 1] if i + 1 < len(parts) else parts[i]
            for i in range(0, len(parts), 2)
        ]
    return parts[0]


def put_row(ref, m, at, dense):
    span = pl.ds(pl.multiple_of(at // SUB * SUB, SUB), SUB)
    here = lax.broadcasted_iota(jnp.int32, (SUB, LANES), 0) == lax.rem(at, SUB)
    for q in range(dense.shape[0]):
        cut = slice(q * LANES, (q + 1) * LANES)
        ref[m, span, cut] = jnp.where(here, dense[q : q + 1], ref[m, span, cut])


def small_row(dots, picks, squares, leading):
    at = lax.broadcasted_iota(jnp.int32, (SUB, LANES), 0)
    extra = jnp.where(at == 0, squares, jnp.where(at == 1, leading, 0.0))
    rest = jnp.zeros((LANES - 2 * SLOTS - SUB, LANES), F32)
    tile = jnp.concatenate([dots, picks, extra, rest], axis=0)
    return jnp.sum(tile.T, axis=0, keepdims=True)


def kernel(
    row_n, col_n, tile_len, w, mats, vx, yu, bid,
    cols, rows, cd, rd, base_c, base_r, row_big, row_small, col_big, col_small,
    load_sem, rows_sem, row_send, row_recv, col_send, col_recv,
    first_send, first_recv, cols_send, cols_recv, rows_send, rows_recv,
):
    batch_n, height, pieces, _ = w.shape
    blocks = height // LANES
    row_place = lax.axis_index("row")
    col_place = lax.axis_index("col")
    row_peers = peers("row", row_n)
    col_peers = peers("col", col_n)

    def load(m, q):
        return pltpu.make_async_copy(
            w.at[m, :, q, :], mats.at[m, :, q * LANES : (q + 1) * LANES], load_sem.at[m, q]
        )

    def load_rows(m):
        return pltpu.make_async_copy(w.at[m, pl.ds(0, ROWS_KEPT)], rows.at[m], rows_sem.at[m])

    for m in range(batch_n):
        load(m, 0).start()

    @pl.when(row_place == 0)
    def _():
        for m in range(batch_n):
            load_rows(m).start()

    for m in range(batch_n):
        for q in range(1, pieces):
            load(m, q).start()

    vx[...] = jnp.zeros_like(vx)
    yu[...] = jnp.zeros_like(yu)
    bid[...] = jnp.zeros_like(bid)
    rd[...] = jnp.zeros_like(rd)
    col_big[...] = jnp.zeros_like(col_big)
    col_small[...] = jnp.zeros_like(col_small)

    barrier = pltpu.get_barrier_semaphore()
    for axis, count, others in (("row", row_n, row_peers), ("col", col_n, col_peers)):
        for to, _ in others:
            pl.semaphore_signal(barrier, inc=1, device_id={axis: to}, device_id_type=MESH)
    pl.semaphore_wait(barrier, row_n + col_n - 2)

    def remote(ref, send, recv, axis, to):
        return pltpu.make_async_remote_copy(
            src_ref=ref,
            dst_ref=ref,
            send_sem=send,
            recv_sem=recv,
            device_id={axis: to},
            device_id_type=MESH,
        )

    def first_col(at, to):
        return remote(cols.at[:, 0], first_send.at[at], first_recv, "col", to)

    def later_cols(at, to):
        return remote(
            cols.at[:, pl.ds(1, TOTAL)], cols_send.at[at], cols_recv, "col", to
        )

    def row_copy(m, k, at, to):
        return remote(rows.at[m, k], rows_send.at[m, at], rows_recv.at[m, k], "row", to)

    for m in range(batch_n):
        load(m, 0).wait()

    @pl.when(col_place == 0)
    def _():
        for m in range(batch_n):
            for b in range(blocks):
                turned = mats[m, b * LANES : (b + 1) * LANES, 0:LANES].T
                for j in range(TOTAL + 1):
                    cols[m, j, b : b + 1, :] = turned[j : j + 1]
        for at, (to, _) in enumerate(col_peers):
            first_col(at, to).start()
        for at, (to, _) in enumerate(col_peers):
            later_cols(at, to).start()

    @pl.when(row_place == 0)
    def _():
        for m in range(batch_n):
            load_rows(m).wait()
            for at, (to, _) in enumerate(row_peers):
                row_copy(m, 0, at, to).start()

    @pl.when(col_place != 0)
    def _():
        first_col(0, 0).wait_recv()

    grow = row_ids(blocks, tile_len, row_n, row_place)
    gcol = col_ids(pieces, tile_len, col_n, col_place)
    lane = lax.broadcasted_iota(jnp.int32, (1, LANES), 1)
    own_row = jnp.where(row_place == 0, lane, -1)
    own_col = jnp.where(col_place == 0, lane, -1)
    row_at = lax.broadcasted_iota(jnp.int32, (SUB, LANES), 0)
    lane_at = lax.broadcasted_iota(jnp.int32, (SUB, LANES), 1)

    def exchange(axis, others, par, m, which, ref, sems):
        me = lax.axis_index(axis)
        send, recv = sems
        span = pl.ds(me, 1) if which == 0 else me
        sends = [
            remote(ref.at[par, m, span], send.at[m, which, at], recv.at[par, m, which, me], axis, to)
            for at, (to, _) in enumerate(others)
        ]
        return sends

    def arrivals(axis, others, par, m, which, ref, sems):
        send, recv = sems
        return [
            remote(
                ref.at[par, m, pl.ds(source, 1) if which == 0 else source],
                send.at[m, which, at],
                recv.at[par, m, which, source],
                axis,
                source,
            )
            for at, (_, source) in enumerate(others)
        ]

    row_args = ("row", row_peers)
    col_args = ("col", col_peers)
    row_sems = (row_send, row_recv)
    col_sems = (col_send, col_recv)

    def take(args, par, m, which, ref, sems):
        for copy in arrivals(*args, par, m, which, ref, sems):
            copy.wait_recv()
        for copy in exchange(*args, par, m, which, ref, sems):
            copy.wait_send()

    def sums_of(ref, par, m):
        total = jnp.sum(ref[par, m], axis=0, keepdims=True)
        turned = jnp.broadcast_to(total, (LANES, LANES)).T
        dots = turned[0:SLOTS]
        picks = turned[SLOTS : 2 * SLOTS]
        squares = turned[2 * SLOTS : 2 * SLOTS + 1]
        leading = turned[2 * SLOTS + 1 : 2 * SLOTS + 2]
        divisor, factor, bidiag = reflect(leading, squares)
        remain = 1.0 - leading / divisor
        weight = dots / divisor + picks * remain
        return divisor, factor, bidiag, remain, weight, picks

    def before_col(k, m):
        par = lax.rem(k + 1, 2)

        @pl.when(k > 0)
        def _():
            take(col_args, par, m, 0, col_small, col_sems)

        divisor, factor, bidiag, remain, weight, picks = sums_of(col_small, par, m)
        bid[...] = jnp.where((row_at == m) & (lane_at == SUPER_AT - 1 + k), bidiag, bid[...])
        row_vec = jnp.where(gcol == k, 1.0, rd[m] / divisor)
        row_vec = jnp.where(k > 0, row_vec, 0.0)
        at = jnp.where(k > 0, TOTAL - 1 + k, 0)
        put_row(yu, m, at, row_vec)
        column = cols[m, k]
        for b in range(blocks):
            old = vx[m, :, b * LANES : (b + 1) * LANES]
            base_c[m, 0, b : b + 1, :] = factor * (
                column[b : b + 1] * remain - jnp.sum(weight * old, axis=0, keepdims=True)
            )
            base_c[m, 1, b : b + 1, :] = column[b : b + 1] - jnp.sum(
                picks * old, axis=0, keepdims=True
            )
        base_c[m, 2] = jnp.broadcast_to(factor / divisor, (blocks, LANES))

    def new_col(k, m):
        par = lax.rem(k + 1, 2)

        @pl.when(k > 0)
        def _():
            take(col_args, par, m, 1, col_big, col_sems)

        applied = tree([col_big[par, m, s] for s in range(col_n)])
        image = jnp.where(grow >= k, base_c[m, 2] * applied + base_c[m, 0], 0.0)
        at = jnp.where(k > 0, TOTAL - 1 + k, 0)
        put_row(vx, m, at, image)
        return image

    def col_half(k, m):
        par = lax.rem(k, 2)
        image = new_col(k, m)
        piece = jnp.where(grow >= k, base_c[m, 1] - image, 0.0)
        cd[m] = piece
        dots = tree(
            [
                vx[m, :, b * LANES : (b + 1) * LANES] * piece[b : b + 1]
                for b in range(blocks)
            ]
        )
        picks = jnp.where(own_row == k, vx[m, :, 0:LANES], 0.0)
        squares = jnp.sum(piece * piece, axis=0, keepdims=True)
        leading = jnp.sum(jnp.where(grow == k, piece, 0.0), axis=0, keepdims=True)
        small = small_row(dots, picks, squares, leading)
        total = [None] * pieces
        for b in range(blocks):
            scale = jnp.broadcast_to(cd[m, b : b + 1, :], (LANES, LANES)).T
            for g in range(LANES // SUB):
                span = pl.ds(b * LANES + g * SUB, SUB)
                by = scale[g * SUB : (g + 1) * SUB]
                for q in range(pieces):
                    part = mats[m, span, q * LANES : (q + 1) * LANES] * by
                    total[q] = part if total[q] is None else total[q] + part
            if b == blocks // 2 - 1:
                row_small[par, m, pl.ds(row_place, 1), :] = small
                for copy in exchange(*row_args, par, m, 0, row_small, row_sems):
                    copy.start()
        for q in range(pieces):
            row_big[par, m, row_place, q : q + 1, :] = jnp.sum(total[q], axis=0, keepdims=True)
        for copy in exchange(*row_args, par, m, 1, row_big, row_sems):
            copy.start()

        @pl.when((row_place == 0) & (k < TOTAL - 1))
        def _():
            for at, (to, _) in enumerate(row_peers):
                row_copy(m, k, at, to).wait_send()
            for at, (to, _) in enumerate(row_peers):
                row_copy(m, k + 1, at, to).start()

    def before_row(k, m):
        par = lax.rem(k, 2)
        take(row_args, par, m, 0, row_small, row_sems)

        @pl.when(row_place != 0)
        def _():
            row_copy(m, k, 0, 0).wait_recv()

        divisor, factor, bidiag, remain, weight, picks = sums_of(row_small, par, m)
        bid[...] = jnp.where((row_at == m) & (lane_at == k), bidiag, bid[...])
        col_vec = jnp.where(grow == k, 1.0, cd[m] / divisor)
        put_row(vx, m, k, col_vec)
        row = rows[m, k]
        for q in range(pieces):
            old = yu[m, :, q * LANES : (q + 1) * LANES]
            base_r[m, 0, q : q + 1, :] = factor * (
                row[q : q + 1] * remain - jnp.sum(weight * old, axis=0, keepdims=True)
            )
            base_r[m, 1, q : q + 1, :] = row[q : q + 1] - jnp.sum(
                picks * old, axis=0, keepdims=True
            )
        base_r[m, 2] = jnp.broadcast_to(factor / divisor, (pieces, LANES))

    def row_half(k, m):
        par = lax.rem(k, 2)
        take(row_args, par, m, 1, row_big, row_sems)
        trans = tree([row_big[par, m, s] for s in range(row_n)])
        image = jnp.where(gcol > k, base_r[m, 2] * trans + base_r[m, 0], 0.0)
        put_row(yu, m, k, image)
        piece = jnp.where(gcol > k, base_r[m, 1] - image, 0.0)
        rd[m] = piece
        dots = tree(
            [
                yu[m, :, q * LANES : (q + 1) * LANES] * piece[q : q + 1]
                for q in range(pieces)
            ]
        )
        picks = jnp.where(own_col == k + 1, yu[m, :, 0:LANES], 0.0)
        squares = jnp.sum(piece * piece, axis=0, keepdims=True)
        leading = jnp.sum(jnp.where(gcol == k + 1, piece, 0.0), axis=0, keepdims=True)
        small = small_row(dots, picks, squares, leading)
        scale = [
            jnp.broadcast_to(rd[m, q : q + 1, :], (SUB, LANES)) for q in range(pieces)
        ]
        for b in range(blocks):
            groups = []
            for g in range(LANES // SUB):
                span = pl.ds(b * LANES + g * SUB, SUB)
                groups.append(
                    tree(
                        [
                            mats[m, span, q * LANES : (q + 1) * LANES] * scale[q]
                            for q in range(pieces)
                        ]
                    )
                )
            turned = jnp.concatenate(groups, axis=0).T
            col_big[par, m, col_place, b : b + 1, :] = jnp.sum(turned, axis=0, keepdims=True)
            if b == blocks // 2 - 1:
                col_small[par, m, pl.ds(col_place, 1), :] = small
                for copy in exchange(*col_args, par, m, 0, col_small, col_sems):
                    copy.start()
        for copy in exchange(*col_args, par, m, 1, col_big, col_sems):
            copy.start()

    def step_body(k, carry):
        for m in range(batch_n):

            @pl.when(k == 0)
            def _():
                for q in range(1, pieces):
                    load(m, q).wait()

            before_col(k, m)
            col_half(k, m)
        for m in range(batch_n):
            before_row(k, m)
            row_half(k, m)

        @pl.when((k == 0) & (col_place != 0))
        def _():
            later_cols(0, 0).wait_recv()

        return carry

    lax.fori_loop(0, TOTAL, step_body, 0)
    for m in range(batch_n):
        before_col(TOTAL, m)
        new_col(TOTAL, m)

    @pl.when(col_place == 0)
    def _():
        for at, (to, _) in enumerate(col_peers):
            first_col(at, to).wait_send()
            later_cols(at, to).wait_send()

    @pl.when(row_place == 0)
    def _():
        for m in range(batch_n):
            for at, (to, _) in enumerate(row_peers):
                row_copy(m, TOTAL - 1, at, to).wait_send()


def factor_all(w, row_n, col_n, tile_len):
    batch_n, height, pieces, _ = w.shape
    width = pieces * LANES
    blocks = height // LANES
    whole = pl.BlockSpec(memory_space=pltpu.VMEM)
    return pl.pallas_call(
        functools.partial(kernel, row_n, col_n, tile_len),
        out_shape=(
            jax.ShapeDtypeStruct((batch_n, height, width), F32),
            jax.ShapeDtypeStruct((batch_n, SLOTS, height), F32),
            jax.ShapeDtypeStruct((batch_n, SLOTS, width), F32),
            jax.ShapeDtypeStruct((SUB, LANES), F32),
        ),
        in_specs=[pl.BlockSpec(memory_space=pltpu.HBM)],
        out_specs=(whole, whole, whole, whole),
        scratch_shapes=[
            pltpu.VMEM((batch_n, TOTAL + 1, blocks, LANES), F32),
            pltpu.VMEM((batch_n, ROWS_KEPT, pieces, LANES), F32),
            pltpu.VMEM((batch_n, blocks, LANES), F32),
            pltpu.VMEM((batch_n, pieces, LANES), F32),
            pltpu.VMEM((batch_n, 3, blocks, LANES), F32),
            pltpu.VMEM((batch_n, 3, pieces, LANES), F32),
            pltpu.VMEM((2, batch_n, row_n, pieces, LANES), F32),
            pltpu.VMEM((2, batch_n, row_n, LANES), F32),
            pltpu.VMEM((2, batch_n, col_n, blocks, LANES), F32),
            pltpu.VMEM((2, batch_n, col_n, LANES), F32),
            pltpu.SemaphoreType.DMA((batch_n, pieces)),
            pltpu.SemaphoreType.DMA((batch_n,)),
            pltpu.SemaphoreType.DMA((batch_n, 2, row_n)),
            pltpu.SemaphoreType.DMA((2, batch_n, 2, row_n)),
            pltpu.SemaphoreType.DMA((batch_n, 2, col_n)),
            pltpu.SemaphoreType.DMA((2, batch_n, 2, col_n)),
            pltpu.SemaphoreType.DMA((col_n,)),
            pltpu.SemaphoreType.DMA,
            pltpu.SemaphoreType.DMA((col_n,)),
            pltpu.SemaphoreType.DMA,
            pltpu.SemaphoreType.DMA((batch_n, row_n)),
            pltpu.SemaphoreType.DMA((batch_n, TOTAL)),
        ],
        compiler_params=pltpu.CompilerParams(
            collective_id=0, has_side_effects=True, vmem_limit_bytes=24 * 1024 * 1024
        ),
    )(w)


def update_kernel(row_n, col_n, tile_len, mats, vx, yu, out, left, right, stage, sems):
    batch_n, height, width = mats.shape
    pieces = width // LANES
    blocks = height // LANES
    row_place = lax.axis_index("row")
    col_place = lax.axis_index("col")
    slots = stage.shape[0]
    empty = jnp.zeros((LANES - 4 * SLOTS, LANES), F32)

    def halves(value):
        high = value.astype(jnp.bfloat16).astype(F32)
        return high, value - high

    for m in range(batch_n):
        for b in range(blocks):
            high, low = halves(vx[m, :, b * LANES : (b + 1) * LANES])
            stack = jnp.concatenate([high, high, low, low, empty], axis=0)
            left[m, b * LANES : (b + 1) * LANES, :] = stack.T.astype(jnp.bfloat16)
        for q in range(pieces):
            high, low = halves(yu[m, :, q * LANES : (q + 1) * LANES])
            stack = jnp.concatenate([high, low, high, low, empty], axis=0)
            right[m, :, q * LANES : (q + 1) * LANES] = stack.astype(jnp.bfloat16)

    def copies(at):
        slot = lax.rem(at, slots)
        m = at // blocks
        span = pl.ds(pl.multiple_of(lax.rem(at, blocks) * LANES, LANES), LANES)
        return [
            pltpu.make_async_copy(
                stage.at[slot, :, q * LANES : (q + 1) * LANES],
                out.at[m, span, q, :],
                sems.at[slot, q],
            )
            for q in range(pieces)
        ]

    row_at = lax.broadcasted_iota(jnp.int32, (LANES, LANES), 0)
    lane_at = lax.broadcasted_iota(jnp.int32, (LANES, LANES), 1)

    @pl.loop(0, batch_n * blocks)
    def _(at):
        slot = lax.rem(at, slots)
        m = at // blocks
        block = lax.rem(at, blocks)
        span = pl.ds(pl.multiple_of(block * LANES, LANES), LANES)

        @pl.when(at >= slots)
        def _():
            for copy in copies(at - slots):
                copy.wait()

        for q in range(0, pieces, 2):
            cut = slice(q * LANES, (q + 2) * LANES)
            change = jnp.dot(left[m, span, :], right[m, :, cut], preferred_element_type=F32)
            stage[slot, :, cut] = mats[m, span, cut] - change

        @pl.when(col_place == 0)
        def _():
            stage[slot, :, 0:LANES] = jnp.where(lane_at < TOTAL, 0.0, stage[slot, :, 0:LANES])

        @pl.when((row_place == 0) & (block == 0))
        def _():
            stage[slot, 0:ROWS_KEPT, :] = jnp.where(
                lax.broadcasted_iota(jnp.int32, (ROWS_KEPT, width), 0) < TOTAL,
                0.0,
                stage[slot, 0:ROWS_KEPT, :],
            )

        for copy in copies(at):
            copy.start()

    for at in range(batch_n * blocks - slots, batch_n * blocks):
        for copy in copies(at):
            copy.wait()


def update_all(mats, vx, yu, row_n, col_n, tile_len):
    batch_n, height, width = mats.shape
    pieces = width // LANES
    whole = pl.BlockSpec(memory_space=pltpu.VMEM)
    slots = 4
    return pl.pallas_call(
        functools.partial(update_kernel, row_n, col_n, tile_len),
        out_shape=jax.ShapeDtypeStruct((batch_n, height, pieces, LANES), F32),
        in_specs=[whole, whole, whole],
        out_specs=pl.BlockSpec(memory_space=pltpu.HBM),
        scratch_shapes=[
            pltpu.VMEM((batch_n, height, LANES), jnp.bfloat16),
            pltpu.VMEM((batch_n, LANES, width), jnp.bfloat16),
            pltpu.VMEM((slots, LANES, width), F32),
            pltpu.SemaphoreType.DMA((slots, pieces)),
        ],
        compiler_params=pltpu.CompilerParams(vmem_limit_bytes=24 * 1024 * 1024),
    )(mats, vx, yu)


def per_device(weights):
    batch_n, row_cycles, tile_len, col_cycles, _ = weights.shape
    height = row_cycles * tile_len
    parts = tile_len // LANES
    row_n = lax.axis_size("row")
    col_n = lax.axis_size("col")
    w = weights.reshape(batch_n, row_cycles, tile_len, col_cycles, parts, LANES)
    w = w.transpose(0, 1, 2, 4, 3, 5).reshape(batch_n, height, parts * col_cycles, LANES)
    mats, vx, yu, bid = factor_all(w, row_n, col_n, tile_len)
    out = update_all(mats, vx, yu, row_n, col_n, tile_len)
    out = out.reshape(batch_n, row_cycles, tile_len, parts, col_cycles, LANES)
    trailing = out.transpose(0, 1, 2, 4, 3, 5).reshape(weights.shape)
    return (trailing, bid[:batch_n, :TOTAL], bid[:batch_n, SUPER_AT : SUPER_AT + TOTAL])


def solution(mesh):
    placed = (P(None, None, "row", None, "col"),)
    return jax.shard_map(
        per_device,
        mesh=mesh,
        in_specs=placed,
        out_specs=(P(None, None, "row", None, "col"), P(), P()),
        check_vma=False,
    )
```

time: 255 us -> 126 us (0.49)
  Pallas kernels: 203 us -> 125 us
  local copies, waits for them, and re-layouts: 34.4 us -> 0.64 us
  matrix products: 14.8 us -> 0 us
    pallas_call x1, Pallas kernels: 203 us -> 117 us  [factor_all(): pl.pallas_call(functools.partial(kernel, row_n, col_n, tile_len), out_sha...]
    reshape x1 -> x0, local copies, waits for them, and re-layouts: 18 us -> none  [per_device(): mats = weights.reshape(batch_n, height, width)]
    unnamed x1 -> x0, local copies, waits for them, and re-layouts: 15.8 us -> none
    dot_general x1 -> x0, matrix products: 14.8 us -> none  [per_device(): update = jnp.einsum('mpr,mpc->mrc', vx, yu, precision=lax.Precision.HIGH)]
    pallas_call x0 -> x1, Pallas kernels: none -> 7.99 us  [update_all(): pl.pallas_call(functools.partial(update_kernel, row_n, col_n, tile_len),...]
where the time goes in v1:
time: 126 us
  Pallas kernels  125 us (99%)
    pallas_call x1, Pallas kernels, factor_all(): pl.pallas_call(functools.partial(kernel, row_n, col_n, tile_len), out_sha...  117 us
    pallas_call x1, Pallas kernels, update_all(): pl.pallas_call(functools.partial(update_kernel, row_n, col_n, tile_len),...  7.99 us

profile of v1, /device:TPU:0, one launch (start us, length us, event | category | flops | bytes accessed | tf_op | source)
XLA Modules:
  0.0 126.3 jit_solution(12551065683363202042)
XLA Ops:
  0.6 117.1 %shard_map.38 = (f32[2,1024,2048]{2,1,0:T(8,128)S(1)}, f32[2,24,1024]{2,1,0:T(8,128)S(1)}, f32[2,24,2048]{2,1,0:T(8,128)S(1)}, f32[8,128]{1,0:T(8,128)S(1)}) custom-call(f32[2,1024,16,128]{3,2,1,0:T(8,128)} %bitcast.10), custom_call_target="tpu_custom_call" | custom-call | tf_op jit(solution)/shard_map/pallas_call | solution.py:416
  117.7 8.0 %shard_map.39 = f32[2,1024,16,128]{3,2,1,0:T(8,128)} custom-call(f32[2,1024,2048]{2,1,0:T(8,128)S(1)} %get-tuple-element.7.mats, f32[2,24,1024]{2,1,0:T(8,128)S(1)} %get-tuple-element.8.vx, f32[2,24,2048]{2,1,0:T(8,128)S(1)} %get-tuple-element.9.yu), custom_call_target="tpu_custom_call" | custom-call | tf_op jit(solution)/shard_map/pallas_call | solution.py:537
  125.7 0.6 fusion

commit v2 on v1

--- a/solution.py
+++ b/solution.py
@@ -14,7 +14,6 @@
 LANES = 128
 SUB = 8
 ROWS_KEPT = 16
-SUPER_AT = 64
 MESH = pl.DeviceIdType.MESH
 F32 = jnp.float32
 
@@ -83,7 +82,7 @@
 
 def kernel(
     row_n, col_n, tile_len, w, mats, vx, yu, bid,
-    cols, rows, cd, rd, base_c, base_r, row_big, row_small, col_big, col_small,
+    cols, rows, spread, cd, rd, base_c, base_r, row_big, row_small, col_big, col_small,
     load_sem, rows_sem, row_send, row_recv, col_send, col_recv,
     first_send, first_recv, cols_send, cols_recv, rows_send, rows_recv,
 ):
@@ -182,28 +181,24 @@
     row_at = lax.broadcasted_iota(jnp.int32, (SUB, LANES), 0)
     lane_at = lax.broadcasted_iota(jnp.int32, (SUB, LANES), 1)
 
-    def exchange(axis, others, par, m, which, ref, sems):
+    def post(axis, others, par, m, which, ref, sems):
         me = lax.axis_index(axis)
         send, recv = sems
         span = pl.ds(me, 1) if which == 0 else me
-        sends = [
-            remote(ref.at[par, m, span], send.at[m, which, at], recv.at[par, m, which, me], axis, to)
-            for at, (to, _) in enumerate(others)
-        ]
-        return sends
-
-    def arrivals(axis, others, par, m, which, ref, sems):
+        for to, _ in others:
+            remote(
+                ref.at[par, m, span], send.at[m, which], recv.at[par, m, which], axis, to
+            ).start()
+
+    def all_of(axis, others, par, m, which, ref, sems):
         send, recv = sems
-        return [
-            remote(
-                ref.at[par, m, pl.ds(source, 1) if which == 0 else source],
-                send.at[m, which, at],
-                recv.at[par, m, which, source],
-                axis,
-                source,
-            )
-            for at, (_, source) in enumerate(others)
-        ]
+        return remote(
+            ref.at[par, m, pl.ds(0, len(others))],
+            send.at[m, which],
+            recv.at[par, m, which],
+            axis,
+            others[0][0],
+        )
 
     row_args = ("row", row_peers)
     col_args = ("col", col_peers)
@@ -211,10 +206,11 @@
     col_sems = (col_send, col_recv)
 
     def take(args, par, m, which, ref, sems):
-        for copy in arrivals(*args, par, m, which, ref, sems):
-            copy.wait_recv()
-        for copy in exchange(*args, par, m, which, ref, sems):
-            copy.wait_send()
+        all_of(*args, par, m, which, ref, sems).wait_recv()
+
+    def sent(args, par, m, ref_small, ref_big, sems):
+        all_of(*args, par, m, 0, ref_small, sems).wait_send()
+        all_of(*args, par, m, 1, ref_big, sems).wait_send()
 
     def sums_of(ref, par, m):
         total = jnp.sum(ref[par, m], axis=0, keepdims=True)
@@ -233,10 +229,11 @@
 
         @pl.when(k > 0)
         def _():
+            sent(row_args, par, m, row_small, row_big, row_sems)
             take(col_args, par, m, 0, col_small, col_sems)
 
         divisor, factor, bidiag, remain, weight, picks = sums_of(col_small, par, m)
-        bid[...] = jnp.where((row_at == m) & (lane_at == SUPER_AT - 1 + k), bidiag, bid[...])
+        bid[1] = jnp.where((row_at == m) & (lane_at == k - 1), bidiag, bid[1])
         row_vec = jnp.where(gcol == k, 1.0, rd[m] / divisor)
         row_vec = jnp.where(k > 0, row_vec, 0.0)
         at = jnp.where(k > 0, TOTAL - 1 + k, 0)
@@ -270,6 +267,10 @@
         image = new_col(k, m)
         piece = jnp.where(grow >= k, base_c[m, 1] - image, 0.0)
         cd[m] = piece
+        for b in range(blocks):
+            spread[b * LANES : (b + 1) * LANES, :] = jnp.broadcast_to(
+                cd[m, b : b + 1, :], (LANES, LANES)
+            ).T
         dots = tree(
             [
                 vx[m, :, b * LANES : (b + 1) * LANES] * piece[b : b + 1]
@@ -282,21 +283,18 @@
         small = small_row(dots, picks, squares, leading)
         total = [None] * pieces
         for b in range(blocks):
-            scale = jnp.broadcast_to(cd[m, b : b + 1, :], (LANES, LANES)).T
             for g in range(LANES // SUB):
                 span = pl.ds(b * LANES + g * SUB, SUB)
-                by = scale[g * SUB : (g + 1) * SUB]
+                by = spread[span, :]
                 for q in range(pieces):
                     part = mats[m, span, q * LANES : (q + 1) * LANES] * by
                     total[q] = part if total[q] is None else total[q] + part
             if b == blocks // 2 - 1:
                 row_small[par, m, pl.ds(row_place, 1), :] = small
-                for copy in exchange(*row_args, par, m, 0, row_small, row_sems):
-                    copy.start()
+                post(*row_args, par, m, 0, row_small, row_sems)
         for q in range(pieces):
             row_big[par, m, row_place, q : q + 1, :] = jnp.sum(total[q], axis=0, keepdims=True)
-        for copy in exchange(*row_args, par, m, 1, row_big, row_sems):
-            copy.start()
+        post(*row_args, par, m, 1, row_big, row_sems)
 
         @pl.when((row_place == 0) & (k < TOTAL - 1))
         def _():
@@ -307,6 +305,10 @@
 
     def before_row(k, m):
         par = lax.rem(k, 2)
+        @pl.when(k > 0)
+        def _():
+            sent(col_args, par, m, col_small, col_big, col_sems)
+
         take(row_args, par, m, 0, row_small, row_sems)
 
         @pl.when(row_place != 0)
@@ -314,7 +316,7 @@
             row_copy(m, k, 0, 0).wait_recv()
 
         divisor, factor, bidiag, remain, weight, picks = sums_of(row_small, par, m)
-        bid[...] = jnp.where((row_at == m) & (lane_at == k), bidiag, bid[...])
+        bid[0] = jnp.where((row_at == m) & (lane_at == k), bidiag, bid[0])
         col_vec = jnp.where(grow == k, 1.0, cd[m] / divisor)
         put_row(vx, m, k, col_vec)
         row = rows[m, k]
@@ -365,10 +367,8 @@
             col_big[par, m, col_place, b : b + 1, :] = jnp.sum(turned, axis=0, keepdims=True)
             if b == blocks // 2 - 1:
                 col_small[par, m, pl.ds(col_place, 1), :] = small
-                for copy in exchange(*col_args, par, m, 0, col_small, col_sems):
-                    copy.start()
-        for copy in exchange(*col_args, par, m, 1, col_big, col_sems):
-            copy.start()
+                post(*col_args, par, m, 0, col_small, col_sems)
+        post(*col_args, par, m, 1, col_big, col_sems)
 
     def step_body(k, carry):
         for m in range(batch_n):
@@ -394,6 +394,7 @@
     for m in range(batch_n):
         before_col(TOTAL, m)
         new_col(TOTAL, m)
+        sent(col_args, (TOTAL + 1) % 2, m, col_small, col_big, col_sems)
 
     @pl.when(col_place == 0)
     def _():
@@ -419,13 +420,14 @@
             jax.ShapeDtypeStruct((batch_n, height, width), F32),
             jax.ShapeDtypeStruct((batch_n, SLOTS, height), F32),
             jax.ShapeDtypeStruct((batch_n, SLOTS, width), F32),
-            jax.ShapeDtypeStruct((SUB, LANES), F32),
+            jax.ShapeDtypeStruct((2, SUB, LANES), F32),
         ),
         in_specs=[pl.BlockSpec(memory_space=pltpu.HBM)],
         out_specs=(whole, whole, whole, whole),
         scratch_shapes=[
             pltpu.VMEM((batch_n, TOTAL + 1, blocks, LANES), F32),
             pltpu.VMEM((batch_n, ROWS_KEPT, pieces, LANES), F32),
+            pltpu.VMEM((height, LANES), F32),
             pltpu.VMEM((batch_n, blocks, LANES), F32),
             pltpu.VMEM((batch_n, pieces, LANES), F32),
             pltpu.VMEM((batch_n, 3, blocks, LANES), F32),
@@ -436,10 +438,10 @@
             pltpu.VMEM((2, batch_n, col_n, LANES), F32),
             pltpu.SemaphoreType.DMA((batch_n, pieces)),
             pltpu.SemaphoreType.DMA((batch_n,)),
-            pltpu.SemaphoreType.DMA((batch_n, 2, row_n)),
-            pltpu.SemaphoreType.DMA((2, batch_n, 2, row_n)),
-            pltpu.SemaphoreType.DMA((batch_n, 2, col_n)),
-            pltpu.SemaphoreType.DMA((2, batch_n, 2, col_n)),
+            pltpu.SemaphoreType.DMA((batch_n, 2)),
+            pltpu.SemaphoreType.DMA((2, batch_n, 2)),
+            pltpu.SemaphoreType.DMA((batch_n, 2)),
+            pltpu.SemaphoreType.DMA((2, batch_n, 2)),
             pltpu.SemaphoreType.DMA((col_n,)),
             pltpu.SemaphoreType.DMA,
             pltpu.SemaphoreType.DMA((col_n,)),
@@ -453,13 +455,15 @@
     )(w)
 
 
-def update_kernel(row_n, col_n, tile_len, mats, vx, yu, out, left, right, stage, sems):
+def update_kernel(mats, vx, yu, bid, out, diagonal, superdiag, left, right, stage, sems):
     batch_n, height, width = mats.shape
     pieces = width // LANES
     blocks = height // LANES
     row_place = lax.axis_index("row")
     col_place = lax.axis_index("col")
     slots = stage.shape[0]
+    diagonal[...] = bid[0, 0:batch_n, 0:TOTAL]
+    superdiag[...] = bid[1, 0:batch_n, 0:TOTAL]
     empty = jnp.zeros((LANES - 4 * SLOTS, LANES), F32)
 
     def halves(value):
@@ -529,16 +533,20 @@
             copy.wait()
 
 
-def update_all(mats, vx, yu, row_n, col_n, tile_len):
+def update_all(mats, vx, yu, bid):
     batch_n, height, width = mats.shape
     pieces = width // LANES
     whole = pl.BlockSpec(memory_space=pltpu.VMEM)
     slots = 4
     return pl.pallas_call(
-        functools.partial(update_kernel, row_n, col_n, tile_len),
-        out_shape=jax.ShapeDtypeStruct((batch_n, height, pieces, LANES), F32),
-        in_specs=[whole, whole, whole],
-        out_specs=pl.BlockSpec(memory_space=pltpu.HBM),
+        update_kernel,
+        out_shape=(
+            jax.ShapeDtypeStruct((batch_n, height, pieces, LANES), F32),
+            jax.ShapeDtypeStruct((batch_n, TOTAL), F32),
+            jax.ShapeDtypeStruct((batch_n, TOTAL), F32),
+        ),
+        in_specs=[whole, whole, whole, whole],
+        out_specs=(pl.BlockSpec(memory_space=pltpu.HBM), whole, whole),
         scratch_shapes=[
             pltpu.VMEM((batch_n, height, LANES), jnp.bfloat16),
             pltpu.VMEM((batch_n, LANES, width), jnp.bfloat16),
@@ -546,7 +554,7 @@
             pltpu.SemaphoreType.DMA((slots, pieces)),
         ],
         compiler_params=pltpu.CompilerParams(vmem_limit_bytes=24 * 1024 * 1024),
-    )(mats, vx, yu)
+    )(mats, vx, yu, bid)
 
 
 def per_device(weights):
@@ -558,10 +566,10 @@
     w = weights.reshape(batch_n, row_cycles, tile_len, col_cycles, parts, LANES)
     w = w.transpose(0, 1, 2, 4, 3, 5).reshape(batch_n, height, parts * col_cycles, LANES)
     mats, vx, yu, bid = factor_all(w, row_n, col_n, tile_len)
-    out = update_all(mats, vx, yu, row_n, col_n, tile_len)
+    out, diagonal, superdiag = update_all(mats, vx, yu, bid)
     out = out.reshape(batch_n, row_cycles, tile_len, parts, col_cycles, LANES)
     trailing = out.transpose(0, 1, 2, 4, 3, 5).reshape(weights.shape)
-    return (trailing, bid[:batch_n, :TOTAL], bid[:batch_n, SUPER_AT : SUPER_AT + TOTAL])
+    return (trailing, diagonal, superdiag)
 
 
 def solution(mesh):

time: 126 us -> 122 us (0.968)
  Pallas kernels: 125 us -> 121 us
    pallas_call x1, Pallas kernels: 117 us -> 113 us  [factor_all(): pl.pallas_call(functools.partial(kernel, row_n, col_n, tile_len), out_sha...]
where the time goes in v2:
time: 122 us
  Pallas kernels  121 us (99%)
    pallas_call x1, Pallas kernels, factor_all(): pl.pallas_call(functools.partial(kernel, row_n, col_n, tile_len), out_sha...  113 us
    pallas_call x1, Pallas kernels, update_all(): pl.pallas_call(update_kernel, out_shape=(jax.ShapeDtypeStruct((batch_n, h...  8.55 us

profile of v2, /device:TPU:0, one launch (start us, length us, event | category | flops | bytes accessed | tf_op | source)
XLA Modules:
  0.0 121.9 jit_solution(12075936480609990373)
XLA Ops:
  0.6 112.7 %shard_map.38 = (f32[2,1024,2048]{2,1,0:T(8,128)S(1)}, f32[2,24,1024]{2,1,0:T(8,128)S(1)}, f32[2,24,2048]{2,1,0:T(8,128)S(1)}, f32[2,8,128]{2,1,0:T(8,128)S(1)}) custom-call(f32[2,1024,16,128]{3,2,1,0:T(8,128)} %bitcast.10), custom_call_target="tpu_custom_call" | custom-call | tf_op jit(solution)/shard_map/pallas_call | solution.py:417
  113.3 8.6 %shard_map.39 = (f32[2,1024,16,128]{3,2,1,0:T(8,128)}, f32[2,12]{1,0:T(2,128)}, f32[2,12]{1,0:T(2,128)}) custom-call(f32[2,1024,2048]{2,1,0:T(8,128)S(1)} %get-tuple-element.10.mats, f32[2,24,1024]{2,1,0:T(8,128)S(1)} %get-tuple-element.11.vx, f32[2,24,2048]{2,1,0:T(8,128)S(1)} %get-tuple-element.12.yu, f32[2,8,128]{2,1,0:T(8,128)S(1)} %get-tuple-element.13.bid), custom_call_target="tpu_custom_call" | custom-call | tf_op jit(solution)/shard_map/pallas_call | solution.py:541

commit v3 on v2

--- a/solution.py
+++ b/solution.py
@@ -64,11 +64,11 @@
     return parts[0]
 
 
-def put_row(ref, m, at, dense):
+def put_row(ref, m, at, dense, first=0):
     span = pl.ds(pl.multiple_of(at // SUB * SUB, SUB), SUB)
     here = lax.broadcasted_iota(jnp.int32, (SUB, LANES), 0) == lax.rem(at, SUB)
     for q in range(dense.shape[0]):
-        cut = slice(q * LANES, (q + 1) * LANES)
+        cut = slice((first + q) * LANES, (first + q + 1) * LANES)
         ref[m, span, cut] = jnp.where(here, dense[q : q + 1], ref[m, span, cut])
 
 
@@ -82,7 +82,7 @@
 
 def kernel(
     row_n, col_n, tile_len, w, mats, vx, yu, bid,
-    cols, rows, spread, cd, rd, base_c, base_r, row_big, row_small, col_big, col_small,
+    cols, rows, spread, sums, cd, rd, base_c, base_r, row_big, row_small, col_big, col_small,
     load_sem, rows_sem, row_send, row_recv, col_send, col_recv,
     first_send, first_recv, cols_send, cols_recv, rows_send, rows_recv,
 ):
@@ -95,7 +95,7 @@
 
     def load(m, q):
         return pltpu.make_async_copy(
-            w.at[m, :, q, :], mats.at[m, :, q * LANES : (q + 1) * LANES], load_sem.at[m, q]
+            w.at[m, :, q, :], mats.at[m, :, q * LANES : (q + 1) * LANES], load_sem.at[m, min(q, 1)]
         )
 
     def load_rows(m):
@@ -181,36 +181,33 @@
     row_at = lax.broadcasted_iota(jnp.int32, (SUB, LANES), 0)
     lane_at = lax.broadcasted_iota(jnp.int32, (SUB, LANES), 1)
 
-    def post(axis, others, par, m, which, ref, sems):
+    half = pieces // 2
+
+    def channel(axis, par, m, which):
         me = lax.axis_index(axis)
-        send, recv = sems
-        span = pl.ds(me, 1) if which == 0 else me
+        small, big, sems, others = (
+            (row_small, row_big, (row_send, row_recv), row_peers)
+            if axis == "row"
+            else (col_small, col_big, (col_send, col_recv), col_peers)
+        )
+        ref = small.at[par, m] if which == 0 else big.at[par, m, which - 1]
+        own = ref.at[pl.ds(me, 1)]
+        every = ref.at[pl.ds(0, len(others))]
+        return own, every, (sems[0].at[m, which], sems[1].at[par, m, which]), others
+
+    def post(axis, par, m, which):
+        own, _, sems, others = channel(axis, par, m, which)
         for to, _ in others:
-            remote(
-                ref.at[par, m, span], send.at[m, which], recv.at[par, m, which], axis, to
-            ).start()
-
-    def all_of(axis, others, par, m, which, ref, sems):
-        send, recv = sems
-        return remote(
-            ref.at[par, m, pl.ds(0, len(others))],
-            send.at[m, which],
-            recv.at[par, m, which],
-            axis,
-            others[0][0],
-        )
-
-    row_args = ("row", row_peers)
-    col_args = ("col", col_peers)
-    row_sems = (row_send, row_recv)
-    col_sems = (col_send, col_recv)
-
-    def take(args, par, m, which, ref, sems):
-        all_of(*args, par, m, which, ref, sems).wait_recv()
-
-    def sent(args, par, m, ref_small, ref_big, sems):
-        all_of(*args, par, m, 0, ref_small, sems).wait_send()
-        all_of(*args, par, m, 1, ref_big, sems).wait_send()
+            remote(own, *sems, axis, to).start()
+
+    def take(axis, par, m, which):
+        _, every, sems, others = channel(axis, par, m, which)
+        remote(every, *sems, axis, others[0][0]).wait_recv()
+
+    def sent(axis, par, m, count):
+        for which in range(count):
+            _, every, sems, others = channel(axis, par, m, which)
+            remote(every, *sems, axis, others[0][0]).wait_send()
 
     def sums_of(ref, par, m):
         total = jnp.sum(ref[par, m], axis=0, keepdims=True)
@@ -229,8 +226,8 @@
 
         @pl.when(k > 0)
         def _():
-            sent(row_args, par, m, row_small, row_big, row_sems)
-            take(col_args, par, m, 0, col_small, col_sems)
+            sent("row", par, m, 3)
+            take("col", par, m, 0)
 
         divisor, factor, bidiag, remain, weight, picks = sums_of(col_small, par, m)
         bid[1] = jnp.where((row_at == m) & (lane_at == k - 1), bidiag, bid[1])
@@ -254,9 +251,9 @@
 
         @pl.when(k > 0)
         def _():
-            take(col_args, par, m, 1, col_big, col_sems)
-
-        applied = tree([col_big[par, m, s] for s in range(col_n)])
+            take("col", par, m, 1)
+
+        applied = tree([col_big[par, m, 0, s] for s in range(col_n)])
         image = jnp.where(grow >= k, base_c[m, 2] * applied + base_c[m, 0], 0.0)
         at = jnp.where(k > 0, TOTAL - 1 + k, 0)
         put_row(vx, m, at, image)
@@ -267,10 +264,13 @@
         image = new_col(k, m)
         piece = jnp.where(grow >= k, base_c[m, 1] - image, 0.0)
         cd[m] = piece
-        for b in range(blocks):
+
+        def fill(b):
             spread[b * LANES : (b + 1) * LANES, :] = jnp.broadcast_to(
                 cd[m, b : b + 1, :], (LANES, LANES)
             ).T
+
+        fill(0)
         dots = tree(
             [
                 vx[m, :, b * LANES : (b + 1) * LANES] * piece[b : b + 1]
@@ -281,20 +281,26 @@
         squares = jnp.sum(piece * piece, axis=0, keepdims=True)
         leading = jnp.sum(jnp.where(grow == k, piece, 0.0), axis=0, keepdims=True)
         small = small_row(dots, picks, squares, leading)
-        total = [None] * pieces
-        for b in range(blocks):
-            for g in range(LANES // SUB):
-                span = pl.ds(b * LANES + g * SUB, SUB)
-                by = spread[span, :]
-                for q in range(pieces):
-                    part = mats[m, span, q * LANES : (q + 1) * LANES] * by
-                    total[q] = part if total[q] is None else total[q] + part
-            if b == blocks // 2 - 1:
-                row_small[par, m, pl.ds(row_place, 1), :] = small
-                post(*row_args, par, m, 0, row_small, row_sems)
-        for q in range(pieces):
-            row_big[par, m, row_place, q : q + 1, :] = jnp.sum(total[q], axis=0, keepdims=True)
-        post(*row_args, par, m, 1, row_big, row_sems)
+        for b in range(1, blocks):
+            fill(b)
+        for part in range(2):
+            total = [None] * half
+            for b in range(blocks):
+                for g in range(LANES // SUB):
+                    span = pl.ds(b * LANES + g * SUB, SUB)
+                    by = spread[span, :]
+                    for q in range(half):
+                        at = (part * half + q) * LANES
+                        term = mats[m, span, at : at + LANES] * by
+                        total[q] = term if total[q] is None else total[q] + term
+                if part == 0 and b == blocks // 2 - 1:
+                    row_small[par, m, pl.ds(row_place, 1), :] = small
+                    post("row", par, m, 0)
+            for q in range(half):
+                row_big[par, m, part, row_place, q : q + 1, :] = jnp.sum(
+                    total[q], axis=0, keepdims=True
+                )
+            post("row", par, m, 1 + part)
 
         @pl.when((row_place == 0) & (k < TOTAL - 1))
         def _():
@@ -307,9 +313,9 @@
         par = lax.rem(k, 2)
         @pl.when(k > 0)
         def _():
-            sent(col_args, par, m, col_small, col_big, col_sems)
-
-        take(row_args, par, m, 0, row_small, row_sems)
+            sent("col", par, m, 2)
+
+        take("row", par, m, 0)
 
         @pl.when(row_place != 0)
         def _():
@@ -332,51 +338,62 @@
 
     def row_half(k, m):
         par = lax.rem(k, 2)
-        take(row_args, par, m, 1, row_big, row_sems)
-        trans = tree([row_big[par, m, s] for s in range(row_n)])
-        image = jnp.where(gcol > k, base_r[m, 2] * trans + base_r[m, 0], 0.0)
-        put_row(yu, m, k, image)
-        piece = jnp.where(gcol > k, base_r[m, 1] - image, 0.0)
-        rd[m] = piece
-        dots = tree(
-            [
-                yu[m, :, q * LANES : (q + 1) * LANES] * piece[q : q + 1]
-                for q in range(pieces)
+        dots = squares = leading = None
+        for part in range(2):
+            tiles = slice(part * half, (part + 1) * half)
+            take("row", par, m, 1 + part)
+            trans = tree([row_big[par, m, part, s] for s in range(row_n)])
+            here = gcol[tiles]
+            image = jnp.where(here > k, base_r[m, 2, tiles] * trans + base_r[m, 0, tiles], 0.0)
+            put_row(yu, m, k, image, part * half)
+            piece = jnp.where(here > k, base_r[m, 1, tiles] - image, 0.0)
+            rd[m, tiles] = piece
+            terms = [
+                yu[m, :, (part * half + q) * LANES : (part * half + q + 1) * LANES]
+                * piece[q : q + 1]
+                for q in range(half)
             ]
-        )
-        picks = jnp.where(own_col == k + 1, yu[m, :, 0:LANES], 0.0)
-        squares = jnp.sum(piece * piece, axis=0, keepdims=True)
-        leading = jnp.sum(jnp.where(gcol == k + 1, piece, 0.0), axis=0, keepdims=True)
-        small = small_row(dots, picks, squares, leading)
-        scale = [
-            jnp.broadcast_to(rd[m, q : q + 1, :], (SUB, LANES)) for q in range(pieces)
-        ]
-        for b in range(blocks):
-            groups = []
-            for g in range(LANES // SUB):
-                span = pl.ds(b * LANES + g * SUB, SUB)
-                groups.append(
-                    tree(
-                        [
-                            mats[m, span, q * LANES : (q + 1) * LANES] * scale[q]
-                            for q in range(pieces)
-                        ]
+            dots = tree(terms if part == 0 else [dots] + terms)
+            square = jnp.sum(piece * piece, axis=0, keepdims=True)
+            lead = jnp.sum(jnp.where(here == k + 1, piece, 0.0), axis=0, keepdims=True)
+            squares = square if part == 0 else squares + square
+            leading = lead if part == 0 else leading + lead
+            if part == 1:
+                picks = jnp.where(own_col == k + 1, yu[m, :, 0:LANES], 0.0)
+                small = small_row(dots, picks, squares, leading)
+            scale = [
+                jnp.broadcast_to(rd[m, part * half + q : part * half + q + 1, :], (SUB, LANES))
+                for q in range(half)
+            ]
+            for b in range(blocks):
+                groups = []
+                for g in range(LANES // SUB):
+                    span = pl.ds(b * LANES + g * SUB, SUB)
+                    products = []
+                    for q in range(half):
+                        at = (part * half + q) * LANES
+                        products.append(mats[m, span, at : at + LANES] * scale[q])
+                    if part == 0:
+                        sums[span, :] = tree(products)
+                    else:
+                        groups.append(tree(products) + sums[span, :])
+                if part == 1:
+                    turned = jnp.concatenate(groups, axis=0).T
+                    col_big[par, m, 0, col_place, b : b + 1, :] = jnp.sum(
+                        turned, axis=0, keepdims=True
                     )
-                )
-            turned = jnp.concatenate(groups, axis=0).T
-            col_big[par, m, col_place, b : b + 1, :] = jnp.sum(turned, axis=0, keepdims=True)
-            if b == blocks // 2 - 1:
-                col_small[par, m, pl.ds(col_place, 1), :] = small
-                post(*col_args, par, m, 0, col_small, col_sems)
-        post(*col_args, par, m, 1, col_big, col_sems)
+                    if b == min(2, blocks - 1):
+                        col_small[par, m, pl.ds(col_place, 1), :] = small
+                        post("col", par, m, 0)
+        post("col", par, m, 1)
 
     def step_body(k, carry):
         for m in range(batch_n):
 
             @pl.when(k == 0)
             def _():
-                for q in range(1, pieces):
-                    load(m, q).wait()
+                rest = mats.at[m, :, LANES:]
+                pltpu.make_async_copy(rest, rest, load_sem.at[m, 1]).wait()
 
             before_col(k, m)
             col_half(k, m)
@@ -394,7 +411,7 @@
     for m in range(batch_n):
         before_col(TOTAL, m)
         new_col(TOTAL, m)
-        sent(col_args, (TOTAL + 1) % 2, m, col_small, col_big, col_sems)
+        sent("col", (TOTAL + 1) % 2, m, 2)
 
     @pl.when(col_place == 0)
     def _():
@@ -428,18 +445,19 @@
             pltpu.VMEM((batch_n, TOTAL + 1, blocks, LANES), F32),
             pltpu.VMEM((batch_n, ROWS_KEPT, pieces, LANES), F32),
             pltpu.VMEM((height, LANES), F32),
+            pltpu.VMEM((height, LANES), F32),
             pltpu.VMEM((batch_n, blocks, LANES), F32),
             pltpu.VMEM((batch_n, pieces, LANES), F32),
             pltpu.VMEM((batch_n, 3, blocks, LANES), F32),
             pltpu.VMEM((batch_n, 3, pieces, LANES), F32),
-            pltpu.VMEM((2, batch_n, row_n, pieces, LANES), F32),
+            pltpu.VMEM((2, batch_n, 2, row_n, pieces // 2, LANES), F32),
             pltpu.VMEM((2, batch_n, row_n, LANES), F32),
-            pltpu.VMEM((2, batch_n, col_n, blocks, LANES), F32),
+            pltpu.VMEM((2, batch_n, 1, col_n, blocks, LANES), F32),
             pltpu.VMEM((2, batch_n, col_n, LANES), F32),
-            pltpu.SemaphoreType.DMA((batch_n, pieces)),
+            pltpu.SemaphoreType.DMA((batch_n, 2)),
             pltpu.SemaphoreType.DMA((batch_n,)),
-            pltpu.SemaphoreType.DMA((batch_n, 2)),
-            pltpu.SemaphoreType.DMA((2, batch_n, 2)),
+            pltpu.SemaphoreType.DMA((batch_n, 3)),
+            pltpu.SemaphoreType.DMA((2, batch_n, 3)),
             pltpu.SemaphoreType.DMA((batch_n, 2)),
             pltpu.SemaphoreType.DMA((2, batch_n, 2)),
             pltpu.SemaphoreType.DMA((col_n,)),
@@ -470,15 +488,17 @@
         high = value.astype(jnp.bfloat16).astype(F32)
         return high, value - high
 
-    for m in range(batch_n):
-        for b in range(blocks):
-            high, low = halves(vx[m, :, b * LANES : (b + 1) * LANES])
-            stack = jnp.concatenate([high, high, low, low, empty], axis=0)
-            left[m, b * LANES : (b + 1) * LANES, :] = stack.T.astype(jnp.bfloat16)
+    def put_left(m, b):
+        span = pl.ds(pl.multiple_of(b * LANES, LANES), LANES)
+        high, low = halves(vx[m, :, span])
+        stack = jnp.concatenate([high, high, low, low, empty], axis=0)
+        left[lax.rem(b, 2)] = stack.T.astype(jnp.bfloat16)
+
+    def put_right(m):
         for q in range(pieces):
             high, low = halves(yu[m, :, q * LANES : (q + 1) * LANES])
             stack = jnp.concatenate([high, low, high, low, empty], axis=0)
-            right[m, :, q * LANES : (q + 1) * LANES] = stack.astype(jnp.bfloat16)
+            right[:, q * LANES : (q + 1) * LANES] = stack.astype(jnp.bfloat16)
 
     def copies(at):
         slot = lax.rem(at, slots)
@@ -488,30 +508,34 @@
             pltpu.make_async_copy(
                 stage.at[slot, :, q * LANES : (q + 1) * LANES],
                 out.at[m, span, q, :],
-                sems.at[slot, q],
+                sems.at[slot],
             )
             for q in range(pieces)
         ]
 
-    row_at = lax.broadcasted_iota(jnp.int32, (LANES, LANES), 0)
+    def drain(at):
+        slot = lax.rem(at, slots)
+        pltpu.make_async_copy(stage.at[slot], stage.at[slot], sems.at[slot]).wait()
+
     lane_at = lax.broadcasted_iota(jnp.int32, (LANES, LANES), 1)
 
-    @pl.loop(0, batch_n * blocks)
-    def _(at):
+    def block_body(m, block):
+        at = m * blocks + block
         slot = lax.rem(at, slots)
-        m = at // blocks
-        block = lax.rem(at, blocks)
         span = pl.ds(pl.multiple_of(block * LANES, LANES), LANES)
 
         @pl.when(at >= slots)
         def _():
-            for copy in copies(at - slots):
-                copy.wait()
+            drain(at)
 
         for q in range(0, pieces, 2):
             cut = slice(q * LANES, (q + 2) * LANES)
-            change = jnp.dot(left[m, span, :], right[m, :, cut], preferred_element_type=F32)
+            change = jnp.dot(
+                left[lax.rem(block, 2)], right[:, cut], preferred_element_type=F32
+            )
             stage[slot, :, cut] = mats[m, span, cut] - change
+
+        put_left(m, lax.rem(block + 1, blocks))
 
         @pl.when(col_place == 0)
         def _():
@@ -528,16 +552,20 @@
         for copy in copies(at):
             copy.start()
 
+    for m in range(batch_n):
+        put_left(m, 0)
+        put_right(m)
+        pl.loop(0, blocks)(functools.partial(block_body, m))
+
     for at in range(batch_n * blocks - slots, batch_n * blocks):
-        for copy in copies(at):
-            copy.wait()
+        drain(at)
 
 
 def update_all(mats, vx, yu, bid):
     batch_n, height, width = mats.shape
     pieces = width // LANES
     whole = pl.BlockSpec(memory_space=pltpu.VMEM)
-    slots = 4
+    slots = min(4, batch_n * height // LANES)
     return pl.pallas_call(
         update_kernel,
         out_shape=(
@@ -548,10 +576,10 @@
         in_specs=[whole, whole, whole, whole],
         out_specs=(pl.BlockSpec(memory_space=pltpu.HBM), whole, whole),
         scratch_shapes=[
-            pltpu.VMEM((batch_n, height, LANES), jnp.bfloat16),
-            pltpu.VMEM((batch_n, LANES, width), jnp.bfloat16),
+            pltpu.VMEM((2, LANES, LANES), jnp.bfloat16),
+            pltpu.VMEM((LANES, width), jnp.bfloat16),
             pltpu.VMEM((slots, LANES, width), F32),
-            pltpu.SemaphoreType.DMA((slots, pieces)),
+            pltpu.SemaphoreType.DMA((slots,)),
         ],
         compiler_params=pltpu.CompilerParams(vmem_limit_bytes=24 * 1024 * 1024),
     )(mats, vx, yu, bid)

time: 122 us -> 115 us (0.943)
  Pallas kernels: 121 us -> 114 us
    pallas_call x1, Pallas kernels: 113 us -> 107 us  [factor_all(): pl.pallas_call(functools.partial(kernel, row_n, col_n, tile_len), out_sha...]
where the time goes in v3:
time: 115 us
  Pallas kernels  114 us (99%)
    pallas_call x1, Pallas kernels, factor_all(): pl.pallas_call(functools.partial(kernel, row_n, col_n, tile_len), out_sha...  107 us
    pallas_call x1, Pallas kernels, update_all(): pl.pallas_call(update_kernel, out_shape=(jax.ShapeDtypeStruct((batch_n, h...  7.52 us

profile of v3, /device:TPU:0, one launch (start us, length us, event | category | flops | bytes accessed | tf_op | source)
XLA Modules:
  0.0 115.0 jit_solution(16754732506414673902)
XLA Ops:
  0.6 106.9 %shard_map.38 = (f32[2,1024,2048]{2,1,0:T(8,128)S(1)}, f32[2,24,1024]{2,1,0:T(8,128)S(1)}, f32[2,24,2048]{2,1,0:T(8,128)S(1)}, f32[2,8,128]{2,1,0:T(8,128)S(1)}) custom-call(f32[2,1024,16,128]{3,2,1,0:T(8,128)} %bitcast.10), custom_call_target="tpu_custom_call" | custom-call | tf_op jit(solution)/shard_map/pallas_call | solution.py:434
  107.5 7.5 %shard_map.39 = (f32[2,1024,16,128]{3,2,1,0:T(8,128)}, f32[2,12]{1,0:T(2,128)}, f32[2,12]{1,0:T(2,128)}) custom-call(f32[2,1024,2048]{2,1,0:T(8,128)S(1)} %get-tuple-element.10.mats, f32[2,24,1024]{2,1,0:T(8,128)S(1)} %get-tuple-element.11.vx, f32[2,24,2048]{2,1,0:T(8,128)S(1)} %get-tuple-element.12.yu, f32[2,8,128]{2,1,0:T(8,128)S(1)} %get-tuple-element.13.bid), custom_call_target="tpu_custom_call" | custom-call | tf_op jit(solution)/shard_map/pallas_call | solution.py:569

commit v4 on v3

--- a/solution.py
+++ b/solution.py
@@ -144,8 +144,12 @@
             cols.at[:, pl.ds(1, TOTAL)], cols_send.at[at], cols_recv, "col", to
         )
 
-    def row_copy(m, k, at, to):
-        return remote(rows.at[m, k], rows_send.at[m, at], rows_recv.at[m, k], "row", to)
+    def row_copy(m, k, to):
+        return remote(rows.at[m, k], rows_send.at[m], rows_recv.at[m, k], "row", to)
+
+    def rows_sent(m):
+        every = row_big.at[0, 0, pl.ds(0, 2), pl.ds(0, row_n - 1)]
+        remote(every, rows_send.at[m], rows_recv.at[m, 0], "row", row_peers[0][0]).wait_send()
 
     for m in range(batch_n):
         load(m, 0).wait()
@@ -155,10 +159,17 @@
         for m in range(batch_n):
             for b in range(blocks):
                 turned = mats[m, b * LANES : (b + 1) * LANES, 0:LANES].T
-                for j in range(TOTAL + 1):
-                    cols[m, j, b : b + 1, :] = turned[j : j + 1]
+                cols[m, 0, b : b + 1, :] = turned[0:1]
+                spread[(m * blocks + b) * SUB : (m * blocks + b + 1) * SUB, :] = turned[0:SUB]
+                sums[(m * blocks + b) * SUB : (m * blocks + b + 1) * SUB, :] = turned[SUB : 2 * SUB]
         for at, (to, _) in enumerate(col_peers):
             first_col(at, to).start()
+        for m in range(batch_n):
+            for b in range(blocks):
+                for j in range(1, TOTAL + 1):
+                    held = spread if j < SUB else sums
+                    at = (m * blocks + b) * SUB + j % SUB
+                    cols[m, j, b : b + 1, :] = held[at : at + 1, :]
         for at, (to, _) in enumerate(col_peers):
             later_cols(at, to).start()
 
@@ -166,8 +177,8 @@
     def _():
         for m in range(batch_n):
             load_rows(m).wait()
-            for at, (to, _) in enumerate(row_peers):
-                row_copy(m, 0, at, to).start()
+            for to, _ in row_peers:
+                row_copy(m, 0, to).start()
 
     @pl.when(col_place != 0)
     def _():
@@ -302,13 +313,6 @@
                 )
             post("row", par, m, 1 + part)
 
-        @pl.when((row_place == 0) & (k < TOTAL - 1))
-        def _():
-            for at, (to, _) in enumerate(row_peers):
-                row_copy(m, k, at, to).wait_send()
-            for at, (to, _) in enumerate(row_peers):
-                row_copy(m, k + 1, at, to).start()
-
     def before_row(k, m):
         par = lax.rem(k, 2)
         @pl.when(k > 0)
@@ -319,7 +323,7 @@
 
         @pl.when(row_place != 0)
         def _():
-            row_copy(m, k, 0, 0).wait_recv()
+            row_copy(m, k, 0).wait_recv()
 
         divisor, factor, bidiag, remain, weight, picks = sums_of(row_small, par, m)
         bid[0] = jnp.where((row_at == m) & (lane_at == k), bidiag, bid[0])
@@ -397,6 +401,14 @@
 
             before_col(k, m)
             col_half(k, m)
+
+        @pl.when((row_place == 0) & (k < TOTAL - 1))
+        def _():
+            for m in range(batch_n):
+                rows_sent(m)
+                for to, _ in row_peers:
+                    row_copy(m, k + 1, to).start()
+
         for m in range(batch_n):
             before_row(k, m)
             row_half(k, m)
@@ -422,8 +434,7 @@
     @pl.when(row_place == 0)
     def _():
         for m in range(batch_n):
-            for at, (to, _) in enumerate(row_peers):
-                row_copy(m, TOTAL - 1, at, to).wait_send()
+            rows_sent(m)
 
 
 def factor_all(w, row_n, col_n, tile_len):
@@ -464,7 +475,7 @@
             pltpu.SemaphoreType.DMA,
             pltpu.SemaphoreType.DMA((col_n,)),
             pltpu.SemaphoreType.DMA,
-            pltpu.SemaphoreType.DMA((batch_n, row_n)),
+            pltpu.SemaphoreType.DMA((batch_n,)),
             pltpu.SemaphoreType.DMA((batch_n, TOTAL)),
         ],
         compiler_params=pltpu.CompilerParams(

time: 115 us -> 114 us (level)
    pallas_call x1, Pallas kernels: 107 us -> 106 us  [factor_all(): pl.pallas_call(functools.partial(kernel, row_n, col_n, tile_len), out_sha...]
where the time goes in v4:
time: 114 us
  Pallas kernels  113 us (99%)
    pallas_call x1, Pallas kernels, factor_all(): pl.pallas_call(functools.partial(kernel, row_n, col_n, tile_len), out_sha...  106 us
    pallas_call x1, Pallas kernels, update_all(): pl.pallas_call(update_kernel, out_shape=(jax.ShapeDtypeStruct((batch_n, h...  7.53 us

profile of v4, /device:TPU:0, one launch (start us, length us, event | category | flops | bytes accessed | tf_op | source)
XLA Modules:
  0.0 113.8 jit_solution(9340907210581274387)
XLA Ops:
  0.6 105.6 %shard_map.38 = (f32[2,1024,2048]{2,1,0:T(8,128)S(1)}, f32[2,24,1024]{2,1,0:T(8,128)S(1)}, f32[2,24,2048]{2,1,0:T(8,128)S(1)}, f32[2,8,128]{2,1,0:T(8,128)S(1)}) custom-call(f32[2,1024,16,128]{3,2,1,0:T(8,128)} %bitcast.10), custom_call_target="tpu_custom_call" | custom-call | tf_op jit(solution)/shard_map/pallas_call | solution.py:445
  106.2 7.5 %shard_map.39 = (f32[2,1024,16,128]{3,2,1,0:T(8,128)}, f32[2,12]{1,0:T(2,128)}, f32[2,12]{1,0:T(2,128)}) custom-call(f32[2,1024,2048]{2,1,0:T(8,128)S(1)} %get-tuple-element.10.mats, f32[2,24,1024]{2,1,0:T(8,128)S(1)} %get-tuple-element.11.vx, f32[2,24,2048]{2,1,0:T(8,128)S(1)} %get-tuple-element.12.yu, f32[2,8,128]{2,1,0:T(8,128)S(1)} %get-tuple-element.13.bid), custom_call_target="tpu_custom_call" | custom-call | tf_op jit(solution)/shard_map/pallas_call | solution.py:580

commit v5 on v4

--- a/solution.py
+++ b/solution.py
@@ -103,6 +103,12 @@
 
     for m in range(batch_n):
         load(m, 0).start()
+    col_big[...] = jnp.zeros_like(col_big)
+    col_small[...] = jnp.zeros_like(col_small)
+    barrier = pltpu.get_barrier_semaphore()
+    for axis, others in (("row", row_peers), ("col", col_peers)):
+        for to, _ in others:
+            pl.semaphore_signal(barrier, inc=1, device_id={axis: to}, device_id_type=MESH)
 
     @pl.when(row_place == 0)
     def _():
@@ -117,13 +123,6 @@
     yu[...] = jnp.zeros_like(yu)
     bid[...] = jnp.zeros_like(bid)
     rd[...] = jnp.zeros_like(rd)
-    col_big[...] = jnp.zeros_like(col_big)
-    col_small[...] = jnp.zeros_like(col_small)
-
-    barrier = pltpu.get_barrier_semaphore()
-    for axis, count, others in (("row", row_n, row_peers), ("col", col_n, col_peers)):
-        for to, _ in others:
-            pl.semaphore_signal(barrier, inc=1, device_id={axis: to}, device_id_type=MESH)
     pl.semaphore_wait(barrier, row_n + col_n - 2)
 
     def remote(ref, send, recv, axis, to):
@@ -484,15 +483,19 @@
     )(w)
 
 
-def update_kernel(mats, vx, yu, bid, out, diagonal, superdiag, left, right, stage, sems):
+def update_kernel(
+    mats, vx, yu, bid, out, diagonal, superdiag, left, right, stage, ends, sems, end_sems
+):
     batch_n, height, width = mats.shape
     pieces = width // LANES
     blocks = height // LANES
     row_place = lax.axis_index("row")
     col_place = lax.axis_index("col")
     slots = stage.shape[0]
-    diagonal[...] = bid[0, 0:batch_n, 0:TOTAL]
-    superdiag[...] = bid[1, 0:batch_n, 0:TOTAL]
+    finals = []
+    for at, ref in enumerate((diagonal, superdiag)):
+        ends[at] = bid[at, 0:batch_n, 0:TOTAL]
+        finals.append(pltpu.make_async_copy(ends.at[at], ref, end_sems.at[at]))
     empty = jnp.zeros((LANES - 4 * SLOTS, LANES), F32)
 
     def halves(value):
@@ -566,10 +569,15 @@
     for m in range(batch_n):
         put_left(m, 0)
         put_right(m)
+        if m == 0:
+            for copy in finals:
+                copy.start()
         pl.loop(0, blocks)(functools.partial(block_body, m))
 
     for at in range(batch_n * blocks - slots, batch_n * blocks):
         drain(at)
+    for copy in finals:
+        copy.wait()
 
 
 def update_all(mats, vx, yu, bid):
@@ -585,12 +593,14 @@
             jax.ShapeDtypeStruct((batch_n, TOTAL), F32),
         ),
         in_specs=[whole, whole, whole, whole],
-        out_specs=(pl.BlockSpec(memory_space=pltpu.HBM), whole, whole),
+        out_specs=(pl.BlockSpec(memory_space=pltpu.HBM),) * 3,
         scratch_shapes=[
             pltpu.VMEM((2, LANES, LANES), jnp.bfloat16),
             pltpu.VMEM((LANES, width), jnp.bfloat16),
             pltpu.VMEM((slots, LANES, width), F32),
+            pltpu.VMEM((2, batch_n, TOTAL), F32),
             pltpu.SemaphoreType.DMA((slots,)),
+            pltpu.SemaphoreType.DMA((2,)),
         ],
         compiler_params=pltpu.CompilerParams(vmem_limit_bytes=24 * 1024 * 1024),
     )(mats, vx, yu, bid)

time: 114 us -> 113 us (level)
  no operation moved by 1% of the time
where the time goes in v5:
time: 113 us
  Pallas kernels  113 us (100%)
    pallas_call x1, Pallas kernels, factor_all(): pl.pallas_call(functools.partial(kernel, row_n, col_n, tile_len), out_sha...  106 us
    pallas_call x1, Pallas kernels, update_all(): pl.pallas_call(update_kernel, out_shape=(jax.ShapeDtypeStruct((batch_n, h...  6.97 us

profile of v5, /device:TPU:0, one launch (start us, length us, event | category | flops | bytes accessed | tf_op | source)
XLA Modules:
  0.0 113.2 jit_solution(17263528035951210781)
XLA Ops:
  0.6 105.6 %shard_map.38 = (f32[2,1024,2048]{2,1,0:T(8,128)S(1)}, f32[2,24,1024]{2,1,0:T(8,128)S(1)}, f32[2,24,2048]{2,1,0:T(8,128)S(1)}, f32[2,8,128]{2,1,0:T(8,128)S(1)}) custom-call(f32[2,1024,16,128]{3,2,1,0:T(8,128)} %bitcast.10), custom_call_target="tpu_custom_call" | custom-call | tf_op jit(solution)/shard_map/pallas_call | solution.py:444
  106.2 7.0 %shard_map.39 = (f32[2,1024,16,128]{3,2,1,0:T(8,128)}, f32[2,12]{1,0:T(2,128)}, f32[2,12]{1,0:T(2,128)}) custom-call(f32[2,1024,2048]{2,1,0:T(8,128)S(1)} %get-tuple-element.10.mats, f32[2,24,1024]{2,1,0:T(8,128)S(1)} %get-tuple-element.11.vx, f32[2,24,2048]{2,1,0:T(8,128)S(1)} %get-tuple-element.12.yu, f32[2,8,128]{2,1,0:T(8,128)S(1)} %get-tuple-element.13.bid), custom_call_target="tpu_custom_call" | custom-call | tf_op jit(solution)/shard_map/pallas_call | solution.py:588
